TPU v7x, 256 devices: a whole 4x4x8 slice. The times are simulated.
256 devices in a mesh: row: 8 (over x, y_hi), col: 32 (over z, y_lo, core).
Axes of the slice: x: 4, y: 4 (y_hi: 2, y_lo: 2; y = y_hi * 2 + y_lo), z: 8, core: 2. Of those that a mesh axis runs over, the one named last changes fastest.
Arguments:
- grams: bfloat16 [4, 8, 32, 32, 8192], P(None, None, 'col', None, 'row'), may hold values from -2.6 to 32, as said below
- adjusted: bfloat16 [4, 8192, 1024], P(None, ('row', 'col')), may hold values from -6 to 6
Outputs:
- merged: float32 [8192, 1024], P(('row', 'col'))
- residual_norms: float32 [3], replicated
Inputs may be any that keep to these rules, and one draw needn't show every extreme that they name: `grams`: each G_m is symmetric positive definite.
All inputs are finite; a program needn't handle non-finite values.
Results may differ from a plain program's by a relative error of at most 0.0041.
Values may be sent and summed in bfloat16 or wider, within the bound.
A program may use at most 64 MiB of HBM per device.

v0:
```python
import jax
import jax.numpy as jnp
from jax import lax
from jax.sharding import Mesh
from jax.sharding import PartitionSpec as P

SWEEPS = 3
COL = ("col_0", "col_1", "col_2")
ROW = ("row_0", "row_1")
ROW_COL = ("row_0", "row_1", "col_0", "col_1", "col_2")


SHRINK = 0.9


def split_up(value, dim, peers):
    dims = value.shape
    tiles = value.reshape(*dims[:dim], peers, dims[dim] // peers, *dims[dim + 1 :])
    return jnp.moveaxis(tiles, dim, 0)


def sum_at_owner(value, axis, dim):
    tiles = split_up(value, dim, lax.axis_size(axis))
    arrived = lax.all_to_all(tiles, axis, split_axis=0, concat_axis=0, tiled=True)
    return arrived.sum(axis=0)


def one_axis_at_a_time(value, axes):
    for axis in axes:
        value = lax.psum(value, axis)
    return value


def block_solve(factor, rows):
    lower = lax.linalg.triangular_solve(factor, rows, left_side=True, lower=True)
    return lax.linalg.triangular_solve(factor, lower, left_side=True, lower=True, transpose_a=True)


def apply_gram(gram_flat, operand):
    panels = lax.all_gather(operand, COL, axis=1, tiled=True)
    partial_value = lax.slice_in_dim(gram_flat, 0, operand.shape[1] * lax.axis_size(ROW), axis=1)
    return sum_at_owner(
        jnp.einsum("ksi,kio->so", partial_value, panels, preferred_element_type=jnp.float32), ROW, 0
    )


def local(grams, adjusted):
    models = grams.shape[0]
    major = grams.shape[1]
    sub_rows = grams.shape[3]
    columns = grams.shape[4]
    here_row = lax.axis_index(ROW)
    here_col = lax.axis_index(COL)
    gram_flat = grams.reshape(models, major * sub_rows, columns)
    total32 = jnp.sum(grams.astype(jnp.float32), axis=0)
    gram_total = total32.astype(jnp.bfloat16).reshape(1, major * sub_rows, columns)
    own_rows = lax.dynamic_slice_in_dim(grams[:, :, 0], here_row, 1, 1)[:, 0]
    own_block = lax.dynamic_slice_in_dim(own_rows, here_col * sub_rows, sub_rows, 2).astype(
        jnp.float32
    )
    diag_each = jnp.diagonal(own_block, axis1=1, axis2=2)
    diag_sum = jnp.sum(diag_each, 0)
    precond = SHRINK * jnp.sum(own_block, 0) + (1.0 - SHRINK) * jnp.diag(diag_sum)
    factor = jnp.linalg.cholesky(precond)
    weights32 = adjusted.astype(jnp.float32)
    rhs = SHRINK * apply_gram(gram_flat, adjusted)
    rhs = rhs + (1.0 - SHRINK) * jnp.sum(diag_each[:, :, None] * weights32, 0)
    rhs_local = jnp.sum(rhs * rhs)
    merged = jnp.mean(weights32, 0)
    squares_list = []
    for sweep_index in range(SWEEPS):
        image = SHRINK * apply_gram(gram_total, merged.astype(jnp.bfloat16)[None])
        image = image + (1.0 - SHRINK) * diag_sum[:, None] * merged
        resid = rhs - image
        squares_local = jnp.sum(resid * resid)
        squares_list.append(squares_local)
        merged = merged + block_solve(factor, resid)
    totals = one_axis_at_a_time(jnp.stack(squares_list + [rhs_local]), ROW_COL)
    norms = jnp.sqrt(totals[:SWEEPS] / totals[SWEEPS])
    return (merged, norms)


def solution(mesh):
    finer = Mesh(mesh.devices.reshape(4, 2, 8, 2, 2), ("row_0", "row_1", "col_0", "col_1", "col_2"))
    placed = (P(None, None, COL, None, ROW), P(None, ROW_COL, None))
    return jax.shard_map(
        local, mesh=finer, in_specs=placed, out_specs=(P(ROW_COL, None), P()), check_vma=False
    )
```

profile of v0, /device:TPU:1, one launch (start us, length us, event | category | flops | bytes accessed | tf_op | source)
XLA Modules:
  0.0 421.2 jit_solution(12293854520328392393)
XLA Ops:
  7.2 0.0 copy-start
  7.2 0.0 all-gather.10.cloned.1.call-start
  7.3 1.5 copy-done
  8.8 0.1 constant_dynamic-slice_fusion
  8.9 0.3 copy.16
  9.2 0.1 convert_bitcast_fusion
  9.2 0.7 gather_fusion
  9.9 0.1 copy.14
  10.0 1.1 convert_reduce_fusion.1
  11.1 0.6 multiply_convert_fusion
  11.8 0.0 all-gather.10.cloned.1.call-update
  11.8 0.0 all-gather.8.cloned.1.call-start
  11.8 0.7 all-gather.8.cloned.1.call-update
  12.5 0.4 reduce_sum.125
  13.0 67.6 %all-gather.10.cloned.1.call-done = bf16[1024,1024]{1,0:T(8,128)(2,1)} async-done(((bf16[32,1024]{1,0:T(8,128)(2,1)}), bf16[1024,1024]{1,0:T(8,128)(2,1)}) %all-gather.10.cloned.1.call-update) | async-done | bytes 2097168 | tf_op jit(solution)/shard_map/all_gather | solution.py:40
  80.5 3.3 fusion.7
  83.8 6.1 %all-to-all-start.1 = ((f32[8,32,1024]{2,1,0:T(8,128)}), f32[8,32,1024]{2,1,0:T(8,128)}, u32[]{:S(2)}, u32[]{:S(2)}) async-start(f32[8,32,1024]{2,1,0:T(8,128)} %fusion.7), calls=%async_computation.1 | async-start | bytes 2097152 | tf_op jit(solution)/shard_map/all_to_all | solution.py:24
  89.9 0.2 convert_reduce_fusion
  90.2 0.1 copy.12
  90.2 67.5 %all-gather.8.cloned.1.call-done = bf16[4,1024,1024]{2,1,0:T(8,128)(2,1)} async-done(((bf16[4,32,1024]{2,1,0:T(8,128)(2,1)}), bf16[4,1024,1024]{2,1,0:T(8,128)(2,1)}) %all-gather.8.cloned.1.call-update) | async-done | bytes 8388624 | tf_op jit(solution)/shard_map/all_gather | solution.py:40
  157.7 6.7 %fusion.9 = f32[8,32,1024]{2,1,0:T(8,128)} fusion(bf16[4,1024,1024]{2,1,0:T(8,128)(2,1)} %all-gather.8.cloned.1.call-done, bf16[4,8,1,32,1024]{4,3,2,1,0:T(8,128)(2,1)S(1)} %copy-done), kind=kOutput, calls=%fused_computation.10 | convolution fusion | flops 2147483648 | bytes 11534336 | tf_op jit(solution)/shard_map/ksi,kio->so/dot_general | solution.py:43
  164.4 0.0 all-to-all-done.1
  164.4 7.1 %all-to-all-start = ((f32[8,32,1024]{2,1,0:T(8,128)}), f32[8,32,1024]{2,1,0:T(8,128)}, u32[]{:S(2)}, u32[]{:S(2)}) async-start(f32[8,32,1024]{2,1,0:T(8,128)} %fusion.9), calls=%async_computation | async-start | bytes 2097152 | tf_op jit(solution)/shard_map/all_to_all | solution.py:24
  171.5 0.0 all-gather.12.cloned.1.call-start
  171.6 0.1 copy.13
  171.6 0.1 reduce_sum.122
  171.8 0.1 fusion.26
  171.8 2.9 cholesky.19
  174.8 0.6 compare_reduce_fusion
  175.4 0.7 fusion.15
  176.1 2.4 custom-call.16
  178.5 0.0 copy-start.1
  178.5 1.3 reduce_sum.126
  179.9 7.6 %all-to-all-done = f32[8,32,1024]{2,1,0:T(8,128)} async-done(((f32[8,32,1024]{2,1,0:T(8,128)}), f32[8,32,1024]{2,1,0:T(8,128)}, u32[]{:S(2)}, u32[]{:S(2)}) %all-to-all-start) | async-done | bytes 1048608 | tf_op jit(solution)/shard_map/all_to_all | solution.py:24
  187.5 1.3 reduce_sum.123
  188.8 0.7 multiply_reduce_fusion.3
  189.5 0.3 fusion.22
  189.8 0.9 fusion.27
  190.7 0.0 all-gather.12.cloned.1.call-update
  190.7 0.0 all-gather.14.cloned.1.call-start
  190.8 62.2 %all-gather.12.cloned.1.call-done = bf16[1024,1024]{1,0:T(8,128)(2,1)} async-done(((bf16[32,1024]{1,0:T(8,128)(2,1)}), bf16[1024,1024]{1,0:T(8,128)(2,1)}) %all-gather.12.cloned.1.call-update) | async-done | bytes 2097168 | tf_op jit(solution)/shard_map/all_gather | solution.py:40
  253.0 2.3 fusion.5
  255.3 21.7 %all_to_all.20 = f32[8,32,1024]{2,1,0:T(8,128)} all-to-all(f32[8,32,1024]{2,1,0:T(8,128)S(1)} %fusion.5), channel_id=1, replica_groups=mesh['row_0'=4,'row_1'=2,'col_0'=8,'col_1'=2,'col_2'=2] {'row_0','row_1'}, dimensions={0} | all-to-all | bytes 2097152 | tf_op jit(solution)/shard_map/all_to_all | solution.py:24
  277.0 1.3 reduce_sum.127
  278.3 0.0 copy-done.1
  278.3 0.7 multiply_reduce_fusion.2
  279.0 0.3 fusion.19
  279.3 0.9 fusion.28
  280.2 0.0 all-gather.14.cloned.1.call-update
  280.2 62.7 %all-gather.14.cloned.1.call-done = bf16[1024,1024]{1,0:T(8,128)(2,1)} async-done(((bf16[32,1024]{1,0:T(8,128)(2,1)}), bf16[1024,1024]{1,0:T(8,128)(2,1)}) %all-gather.14.cloned.1.call-update) | async-done | bytes 2097168 | tf_op jit(solution)/shard_map/all_gather | solution.py:40
  342.9 2.3 fusion.3
  345.2 21.6 %all_to_all.21 = f32[8,32,1024]{2,1,0:T(8,128)S(1)} all-to-all(f32[8,32,1024]{2,1,0:T(8,128)S(1)} %fusion.3), channel_id=1, replica_groups=mesh['row_0'=4,'row_1'=2,'col_0'=8,'col_1'=2,'col_2'=2] {'row_0','row_1'}, dimensions={0} | all-to-all | bytes 2097152 | tf_op jit(solution)/shard_map/all_to_all | solution.py:24
  366.8 0.1 reduce_sum.128
  366.9 1.4 multiply_reduce_fusion.1
  368.3 2.7 pad_maximum_fusion
  371.0 6.9 %psum.35 = f32[4]{0:T(128)S(1)} all-reduce(f32[4]{0:T(128)S(1)} %pad_maximum_fusion), channel_id=1, replica_groups=mesh['row_0'=4,'row_1'=2,'col_0'=8,'col_1'=2,'col_2'=2] {'row_0'}, use_global_device_ids=true, to_apply=%region_15.18 | all-reduce | flops 4 | bytes 32 | tf_op jit(solution)/shard_map/psum | solution.py:30
  377.9 5.3 %psum.36 = f32[4]{0:T(128)S(1)} all-reduce(f32[4]{0:T(128)S(1)} %psum.35), channel_id=1, replica_groups=mesh['row_0'=4,'row_1'=2,'col_0'=8,'col_1'=2,'col_2'=2] {'row_1'}, use_global_device_ids=true, to_apply=%region_16.19 | all-reduce | flops 4 | bytes 32 | tf_op jit(solution)/shard_map/psum | solution.py:30
  383.1 12.5 %psum.37 = f32[4]{0:T(128)S(1)} all-reduce(f32[4]{0:T(128)S(1)} %psum.36), channel_id=1, replica_groups=mesh['row_0'=4,'row_1'=2,'col_0'=8,'col_1'=2,'col_2'=2] {'col_0'}, use_global_device_ids=true, to_apply=%region_17.20 | all-reduce | flops 4 | bytes 32 | tf_op jit(solution)/shard_map/psum | solution.py:30
  395.7 0.3 fusion.16
  396.0 4.1 psum.38
  400.1 0.9 convolution_add_fusion
  401.0 11.8 %psum.39 = f32[4]{0:T(128)S(1)} all-reduce(f32[4]{0:T(128)S(1)} %psum.38), channel_id=1, replica_groups=mesh['row_0'=4,'row_1'=2,'col_0'=8,'col_1'=2,'col_2'=2] {'col_2'}, use_global_device_ids=true, to_apply=%region_19.22 | all-reduce | flops 4 | bytes 32 | tf_op jit(solution)/shard_map/psum | solution.py:30
  412.8 0.7 slice.17
  413.4 1.2 divide_sqrt_fusion
  (4 shorter events, 0.0 us)
Async XLA Ops:
  7.2 1.6 copy-start
  7.2 73.4 %all-gather.10.cloned.1.call-start = ((), (), s32[]{:S(2)}) async-start(), calls=%async_computation.5 | async-start | bytes 2162688 | tf_op jit(solution)/shard_map/all_gather | solution.py:40
  11.8 146.0 %all-gather.8.cloned.1.call-start = ((), (), s32[]{:S(2)}) async-start(), calls=%async_computation.4 | async-start | bytes 8650752 | tf_op jit(solution)/shard_map/all_gather | solution.py:40
  83.8 80.6 %all-to-all-start.1 = ((f32[8,32,1024]{2,1,0:T(8,128)}), f32[8,32,1024]{2,1,0:T(8,128)}, u32[]{:S(2)}, u32[]{:S(2)}) async-start(f32[8,32,1024]{2,1,0:T(8,128)} %fusion.7), calls=%async_computation.1 | async-start | bytes 2097152 | tf_op jit(solution)/shard_map/all_to_all | solution.py:24
  164.4 23.0 %all-to-all-start = ((f32[8,32,1024]{2,1,0:T(8,128)}), f32[8,32,1024]{2,1,0:T(8,128)}, u32[]{:S(2)}, u32[]{:S(2)}) async-start(f32[8,32,1024]{2,1,0:T(8,128)} %fusion.9), calls=%async_computation | async-start | bytes 2097152 | tf_op jit(solution)/shard_map/all_to_all | solution.py:24
  171.5 81.4 %all-gather.12.cloned.1.call-start = ((), (), s32[]{:S(2)}) async-start(), calls=%async_computation.6 | async-start | bytes 2162688 | tf_op jit(solution)/shard_map/all_gather | solution.py:40
  178.5 99.7 %copy-start.1 = (f32[32]{0:T(128)}, f32[32]{0:T(128)S(1)}, u32[]{:S(2)}) copy-start(f32[32]{0:T(128)S(1)} %get-tuple-element.14) | copy-start | bytes 388
  190.7 152.2 %all-gather.14.cloned.1.call-start = ((), (), s32[]{:S(2)}) async-start(), calls=%async_computation.7 | async-start | bytes 2162688 | tf_op jit(solution)/shard_map/all_gather | solution.py:40
Sparse Core Ops, SparseCore 0:
  11.9 68.5 all-gather.9
  82.4 75.3 all-gather.7
  190.8 62.0 all-gather.11
  280.4 62.5 all-gather.13
where the time goes:
time: 422 us; the launch traced here: 421 us
  waiting for transfers between devices  268 us (64%)
  blocking collectives  83.9 us (20%)
  other arithmetic  20 us (5%)
  matrix products  18.2 us (4%)
  between operations  13.9 us (3%)
  starting transfers between devices  13.4 us (3%)
    all_gather x4, waiting for transfers between devices, apply_gram(): panels = lax.all_gather(operand, COL, axis=1, tiled=True)  260 us
    all_to_all x2, blocking collectives, sum_at_owner(): lax.all_to_all(tiles, axis, split_axis=0, concat_axis=0, tiled=True)  43.3 us
    psum x5, blocking collectives, one_axis_at_a_time(): value = lax.psum(value, axis)  40.5 us
    dot_general x4, matrix products, apply_gram(): jnp.einsum('ksi,kio->so', partial_value, panels, preferred_element_type=j...  14.5 us
    all_to_all x2, starting transfers between devices, sum_at_owner(): lax.all_to_all(tiles, axis, split_axis=0, concat_axis=0, tiled=True)  13.2 us
  transfers between devices with their start and end apart: 6, of which 5 were waited for; matrix products, arithmetic and copies ran while one was open for 4% of the time, Pallas kernels for 0%

commit v1 on v0

v1 whole, which is shorter than its diff:
```python
import jax
import jax.numpy as jnp
from jax import lax
from jax.experimental import pallas as pl
from jax.experimental.pallas import tpu as pltpu
from jax.sharding import Mesh
from jax.sharding import PartitionSpec as P

SWEEPS = 3
COL = ("z", "yl", "core")
ROW = ("x", "yh")
ROW_COL = ROW + COL
NX, NYH, NZ, NYL, NC = 4, 2, 8, 2, 2
NR = NX * NYH
BLK = 32
SUB = 2 * BLK
HALF = 256
CH = 128
SHRINK = 0.9
REST = 1.0 - SHRINK
F32, BF16 = jnp.float32, jnp.bfloat16
MESH_ID = pl.DeviceIdType.MESH
N_AG = 22
HI = lax.Precision.HIGHEST


def kernel(
    g_hbm, w_hbm, out_hbm, norm_ref,
    gbuf, tot, wbuf, mbuf, acc_r, acc_i, m0s, sendb, recvb, pinv, mst, outst, nb_a, nb_b, nb_c,
    ag_s, ag_r, rs_s, rs_r, in_s, in_r, in_l, out_s, out_r, out_l, n_s, n_r,
):
    x, yh = lax.axis_index("x"), lax.axis_index("yh")
    z, yl, core = lax.axis_index("z"), lax.axis_index("yl"), lax.axis_index("core")
    r = x * NYH + yh
    pairs = 1 - core
    rows = gbuf.shape[2]

    def at_z(d):
        return lax.rem(z + d + NZ, NZ)

    def row_peer(j):
        return {"x": lax.rem(x + j // 2, NX), "yh": (yh + j % 2) % 2}

    def rest_peer(e):
        return {"yl": (yl + e // 2) % 2, "core": (core + e % 2) % 2}

    def remote(src, dst, ss, rs, dev):
        return pltpu.make_async_remote_copy(
            src_ref=src, dst_ref=dst, send_sem=ss, recv_sem=rs, device_id=dev, device_id_type=MESH_ID
        )

    barrier = pltpu.get_barrier_semaphore()
    peers = [row_peer(j) for j in range(1, NR)]
    peers += [{"z": at_z(d)} for d in range(1, NZ)]
    peers += [rest_peer(e) for e in range(1, 4)]
    for dev in peers:
        pl.semaphore_signal(barrier, inc=1, device_id=dev, device_id_type=MESH_ID)

    own0 = wbuf.at[z, yl]
    local = []
    for n in range(2):
        lanes = pl.ds(pl.multiple_of(core * 512 + n * HALF, HALF), HALF)
        local.append(
            pltpu.make_async_copy(
                w_hbm.at[:, :, lanes],
                own0.at[n, :, pl.ds(pl.multiple_of(core * BLK, BLK), BLK)],
                in_l.at[n],
            )
        )
    g_local = pltpu.make_async_copy(g_hbm, gbuf.at[core], in_l.at[2])
    for c in local:
        c.start()
    g_local.start()
    pl.semaphore_wait(barrier, len(peers))

    waits = []
    other = {"core": pairs}
    w_in = []
    for n in range(2):
        lanes = pl.ds(pl.multiple_of(pairs * 512 + n * HALF, HALF), HALF)
        dst = own0.at[n, :, pl.ds(pl.multiple_of(core * BLK, BLK), BLK)]
        c = remote(w_hbm.at[:, :, lanes], dst, in_s.at[n], in_r.at[n], other)
        c.start()
        waits.append(c)
        got = own0.at[n, :, pl.ds(pl.multiple_of(pairs * BLK, BLK), BLK)]
        w_in.append(remote(got, got, in_s.at[n], in_r.at[n], other))
    g_out = remote(g_hbm, gbuf.at[core], in_s.at[2], in_r.at[2], other)
    g_out.start()
    waits.append(g_out)
    for c in local:
        c.wait()
    for c in w_in:
        c.wait_recv()

    def gather(buf, s, step):
        count = [0]

        def send(ref, i, dev):
            c = remote(ref, ref, ag_s.at[s, count[0]], ag_r.at[s, i], dev)
            count[0] += 1
            c.start()
            waits.append(c)

        def arrived(ref, i):
            remote(ref, ref, ag_s.at[s, 0], ag_r.at[s, i], {"yl": 1 - yl}).wait_recv()

        up, down, side = {"z": at_z(1)}, {"z": at_z(-1)}, {"yl": 1 - yl}
        own = buf.at[z, yl]
        send(own, 0, up)
        send(own, 4, down)
        send(own, 7, side)
        for h in range(1, 5):
            ref = buf.at[at_z(-h), yl]
            arrived(ref, h - 1)
            if h <= 3:
                send(ref, h, up)
            send(ref.at[1], 15 + h - 1, side)
            if h <= 3:
                ref = buf.at[at_z(h), yl]
                arrived(ref, 4 + h - 1)
                if h <= 2:
                    send(ref, 4 + h, down)
                send(ref.at[1], 19 + h - 1, side)
            d = h - 1
            if d == 0:
                ref = buf.at[z, 1 - yl]
                arrived(ref, 7)
                send(ref.at[0], 8, up)
                send(ref.at[0], 11, down)
                step([z], True)
            else:
                ref = buf.at[at_z(-d), 1 - yl, 0]
                arrived(ref, 8 + d - 1)
                if d <= 2:
                    send(ref, 8 + d, up)
                ref = buf.at[at_z(d), 1 - yl, 0]
                arrived(ref, 11 + d - 1)
                send(ref, 11 + d, down)
                arrived(buf.at[at_z(-d), 1 - yl, 1], 15 + d - 1)
                arrived(buf.at[at_z(d), 1 - yl, 1], 19 + d - 1)
                step([at_z(-d), at_z(d)], False)
        arrived(buf.at[at_z(4), 1 - yl, 0], 14)
        arrived(buf.at[at_z(4), 1 - yl, 1], 18)
        step([at_z(4)], False)

    def scatter(i, value):
        for j in range(1, NR):
            dev = row_peer(j)
            a = dev["x"] * NYH + dev["yh"]
            for n in range(2):
                sendb[i, a, n] = value(a, n).astype(BF16)
            c = remote(sendb.at[i, a], recvb.at[i, j], rs_s.at[i, j], rs_r.at[i, j], dev)
            c.start()
            waits.append(c)

    def reduced(i, value):
        total = [value(r, n) for n in range(2)]
        for j in range(1, NR):
            ref = recvb.at[i, j]
            remote(ref, ref, rs_s.at[i, j], rs_r.at[i, j], row_peer(1)).wait_recv()
            total = [total[n] + recvb[i, j, n].astype(F32) for n in range(2)]
        return total

    def take(acc_ref):
        def value(a, n):
            lines = pl.ds(pl.multiple_of(a * BLK, BLK), BLK)
            return jnp.concatenate([acc_ref[k, n, lines, :] for k in range(2)], axis=0)
        return value

    def prepare():
        g_local.wait()
        remote(gbuf.at[pairs], gbuf.at[pairs], in_s.at[2], in_r.at[2], other).wait_recv()
        acc_r[...] = jnp.zeros_like(acc_r)
        acc_i[...] = jnp.zeros_like(acc_i)

        def sum_rows(i, carry):
            k, lines = i // 8, pl.ds(pl.multiple_of(lax.rem(i, 8) * BLK, BLK), BLK)
            value = gbuf[k, 0, lines, :].astype(F32)
            for m in range(1, 4):
                value = value + gbuf[k, m, lines, :].astype(F32)
            tot[k, lines, :] = value.astype(BF16)
            return carry

        lax.fori_loop(0, 16, sum_rows, 0)

    def columns(zz):
        return pl.ds(pl.multiple_of(zz * CH, CH), CH)

    def first_step(chunks, start):
        if start:
            prepare()
        for zz in chunks:
            def per_half(n, carry):
                rowsw = [wbuf[zz, :, n, m].reshape(CH, HALF) for m in range(4)]
                mean = (
                    rowsw[0].astype(F32) + rowsw[1].astype(F32) + rowsw[2].astype(F32) + rowsw[3].astype(F32)
                ) * 0.25
                m0s[...] = mean.astype(BF16)

                def per_tile(k, carry):
                    value = acc_r[k, n]
                    for m in range(4):
                        value = value + jnp.dot(
                            gbuf[k, m, :, columns(zz)], wbuf[zz, :, n, m].reshape(CH, HALF),
                            preferred_element_type=F32,
                        )
                    acc_r[k, n] = value
                    acc_i[0, k, n] = acc_i[0, k, n] + jnp.dot(
                        tot[k, :, columns(zz)], m0s[...], preferred_element_type=F32
                    )
                    return carry

                return lax.fori_loop(0, 2, per_tile, carry)

            lax.fori_loop(0, 2, per_half, 0)

    def sweep_step(s):
        def step(chunks, start):
            for zz in chunks:
                def per(i, carry):
                    k, n = i // 2, lax.rem(i, 2)
                    acc_i[s, k, n] = acc_i[s, k, n] + jnp.dot(
                        tot[k, :, columns(zz)], mbuf[s - 1, zz, :, n].reshape(CH, HALF),
                        preferred_element_type=F32,
                    )
                    return carry

                lax.fori_loop(0, 4, per, 0)
        return step

    gather(wbuf, 0, first_step)

    take_r = take(acc_r)
    take_i = [take(acc_i.at[s]) for s in range(SWEEPS)]

    def first_value(a, n):
        return take_r(a, n) - take_i[0](a, n)

    scatter(0, first_value)

    lane = lax.broadcasted_iota(jnp.int32, (2, BLK, CH), 2)
    line = lax.broadcasted_iota(jnp.int32, (2, BLK, CH), 1)
    tile = lax.broadcasted_iota(jnp.int32, (2, BLK, CH), 0)
    at = lane - yl * SUB - tile * BLK
    inside = (at >= 0) & (at < BLK)
    lines = pl.ds(pl.multiple_of(r * BLK, BLK), BLK)
    diag_each, block = [], None
    for m in range(4):
        part = jnp.stack([gbuf[k, m, lines, columns(z)] for k in range(2)], axis=0).astype(F32)
        diag_each.append(jnp.sum(jnp.where(at == line, part, 0.0), axis=2, keepdims=True))
        block = part if block is None else block + part
    diag_sum = diag_each[0] + diag_each[1] + diag_each[2] + diag_each[3]
    matrix = jnp.where(inside, SHRINK * block, 0.0) + jnp.where(at == line, REST * diag_sum, 0.0)

    def eliminate(j, mat):
        row = jnp.sum(jnp.where(line == j, mat, 0.0), axis=1, keepdims=True)
        col = jnp.sum(jnp.where(at == j, mat, 0.0), axis=2, keepdims=True)
        piv = jnp.sum(jnp.where(at[:, :1, :] == j, row, 0.0), axis=2, keepdims=True)
        inv = 1.0 / piv
        scaled = row * inv
        new = jnp.where(at == j, 0.0, mat) - col * jnp.where(at[:, :1, :] == j, inv, scaled)
        return jnp.where(line == j, jnp.where(at == j, inv, scaled), new)

    pinv[...] = lax.fori_loop(0, BLK, eliminate, matrix).reshape(SUB, CH)

    diag64 = diag_sum.reshape(SUB, 1)
    own = [wbuf[z, yl, n] for n in range(2)]
    merged, rest = [], []
    for n in range(2):
        w32 = [own[n][m].astype(F32) for m in range(4)]
        merged.append((w32[0] + w32[1] + w32[2] + w32[3]) * 0.25)
        rest.append(sum(diag_each[m].reshape(SUB, 1) * w32[m] for m in range(4)) * REST)

    def solve(resid):
        return jnp.dot(
            pinv[...], jnp.concatenate([resid, resid], axis=0), precision=HI, preferred_element_type=F32
        )

    def squares(parts):
        return jnp.sum(parts[0] * parts[0]) + jnp.sum(parts[1] * parts[1])

    got = reduced(0, first_value)
    resid = [SHRINK * got[n] + rest[n] - REST * diag64 * merged[n] for n in range(2)]
    sums = [squares(resid)]
    for s in range(1, SWEEPS):
        update = [solve(resid[n]) for n in range(2)]
        for n in range(2):
            merged[n] = merged[n] + update[n]
            mbuf[s - 1, z, yl, n] = merged[n].astype(BF16)
        gather(mbuf.at[s - 1], s, sweep_step(s))

        def change(a, n):
            return take_i[s](a, n) - take_i[s - 1](a, n)

        scatter(s, change)
        if s == 1:
            scatter(3, take_r)
        else:
            rhs = reduced(3, take_r)
            sums_rhs = squares([SHRINK * rhs[n] + rest[n] for n in range(2)])
        got = reduced(s, change)
        resid = [resid[n] - SHRINK * got[n] - REST * diag64 * update[n] for n in range(2)]
        sums.append(squares(resid))
    sums.append(sums_rhs)

    index = lax.broadcasted_iota(jnp.int32, (8, 128), 0)
    value = jnp.zeros((8, 128), F32)
    for i in range(4):
        value = jnp.where(index == i, sums[i], value)
    nb_a[r] = value
    for j in range(1, NR):
        c = remote(nb_a.at[r], nb_a.at[r], n_s.at[0, j], n_r.at[0, j], row_peer(j))
        c.start()
        waits.append(c)

    for n in range(2):
        mst[n] = merged[n] + solve(resid[n])
    final = []
    for n in range(2):
        lanes = pl.ds(pl.multiple_of(core * 512 + n * HALF, HALF), HALF)
        src = mst.at[n, pl.ds(pl.multiple_of(pairs * BLK, BLK), BLK)]
        c = remote(src, outst.at[:, lanes], out_s.at[n], out_r.at[n], other)
        c.start()
        waits.append(c)
        src = mst.at[n, pl.ds(pl.multiple_of(core * BLK, BLK), BLK)]
        c = pltpu.make_async_copy(src, out_hbm.at[:, lanes], out_l.at[n])
        c.start()
        final.append(c)
    for n in range(2):
        lanes = pl.ds(pl.multiple_of(pairs * 512 + n * HALF, HALF), HALF)
        remote(outst.at[:, lanes], outst.at[:, lanes], out_s.at[n], out_r.at[n], other).wait_recv()
        c = pltpu.make_async_copy(outst.at[:, lanes], out_hbm.at[:, lanes], out_l.at[2 + n])
        c.start()
        final.append(c)

    def summed(nb, stage, count, index_of, peer_of):
        for j in range(1, count):
            ref = nb.at[index_of(j)]
            remote(ref, ref, n_s.at[stage, j], n_r.at[stage, j], peer_of(1)).wait_recv()
        value = nb[0]
        for j in range(1, count):
            value = value + nb[j]
        return value

    def row_from(j):
        return lax.rem(x + NX - j // 2, NX) * NYH + (yh + j % 2) % 2

    nb_b[z] = summed(nb_a, 0, NR, row_from, row_peer)
    for d in range(1, NZ):
        c = remote(nb_b.at[z], nb_b.at[z], n_s.at[1, d], n_r.at[1, d], {"z": at_z(d)})
        c.start()
        waits.append(c)
    place = yl * 2 + core
    nb_c[place] = summed(nb_b, 1, NZ, lambda d: at_z(-d), lambda d: {"z": at_z(d)})
    for e in range(1, 4):
        c = remote(nb_c.at[place], nb_c.at[place], n_s.at[2, e], n_r.at[2, e], rest_peer(e))
        c.start()
        waits.append(c)

    def rest_from(e):
        return ((yl + e // 2) % 2) * 2 + (core + e % 2) % 2

    totals = summed(nb_c, 2, 4, rest_from, rest_peer)
    norm_ref[...] = jnp.sqrt(totals / totals[3:4, :])
    for c in final:
        c.wait()
    for c in waits:
        c.wait_send()


def local(grams, adjusted):
    models, major, _, sub_rows, columns = grams.shape
    outs = adjusted.shape[2]
    g = grams.reshape(models, major * sub_rows, columns)
    rows = major * sub_rows
    dma = pltpu.SemaphoreType.DMA
    vmem = pltpu.VMEM
    merged, norms = pl.pallas_call(
        kernel,
        out_shape=(
            jax.ShapeDtypeStruct((sub_rows, outs), F32),
            jax.ShapeDtypeStruct((8, 128), F32),
        ),
        in_specs=[pl.BlockSpec(memory_space=pl.ANY)] * 2,
        out_specs=(pl.BlockSpec(memory_space=pl.ANY), pl.BlockSpec(memory_space=pltpu.VMEM)),
        scratch_shapes=[
            vmem((2, models, rows, columns), BF16),
            vmem((2, rows, columns), BF16),
            vmem((NZ, 2, 2, models, SUB, HALF), BF16),
            vmem((2, NZ, 2, 2, SUB, HALF), BF16),
            vmem((2, 2, rows, HALF), F32),
            vmem((SWEEPS, 2, 2, rows, HALF), F32),
            vmem((CH, HALF), BF16),
            vmem((4, NR, 2, SUB, HALF), BF16),
            vmem((4, NR, 2, SUB, HALF), BF16),
            vmem((SUB, CH), F32),
            vmem((2, SUB, HALF), F32),
            vmem((sub_rows, outs), F32),
            vmem((NR, 8, 128), F32),
            vmem((NZ, 8, 128), F32),
            vmem((4, 8, 128), F32),
            dma((3, N_AG)),
            dma((3, N_AG)),
            dma((4, NR)),
            dma((4, NR)),
            dma((3,)),
            dma((3,)),
            dma((3,)),
            dma((2,)),
            dma((2,)),
            dma((4,)),
            dma((3, NR)),
            dma((3, NR)),
        ],
        compiler_params=pltpu.CompilerParams(
            collective_id=0, has_side_effects=True, vmem_limit_bytes=48 * 1024 * 1024
        ),
        name="merge",
    )(g, adjusted)
    return merged, norms[:SWEEPS, 0]


def solution(mesh):
    finer = Mesh(mesh.devices.reshape(NX, NYH, NZ, NYL, NC), ROW_COL)
    placed = (P(None, None, COL, None, ROW), P(None, ROW_COL, None))
    return jax.shard_map(
        local, mesh=finer, in_specs=placed, out_specs=(P(ROW_COL, None), P()), check_vma=False
    )
```

time: 422 us -> 136 us (0.32)
  waiting for transfers between devices: 268 us -> 0 us
  Pallas kernels: 0 us -> 131 us
  blocking collectives: 83.9 us -> 0 us
  other arithmetic: 20 us -> 0 us
  matrix products: 18.2 us -> 0 us
  starting transfers between devices: 13.4 us -> 0 us
  between operations: 13.9 us -> 0.65 us
    all_gather x4 -> x0, waiting for transfers between devices: 260 us -> none  [apply_gram(): panels = lax.all_gather(operand, COL, axis=1, tiled=True)]
    pallas_call x0 -> x1, Pallas kernels: none -> 131 us  [local(): pl.pallas_call(kernel, out_shape=(jax.ShapeDtypeStruct((sub_rows, outs),...]
    all_to_all x2 -> x0, blocking collectives: 43.3 us -> none  [sum_at_owner(): lax.all_to_all(tiles, axis, split_axis=0, concat_axis=0, tiled=True)]
    psum x5 -> x0, blocking collectives: 40.5 us -> none  [one_axis_at_a_time(): value = lax.psum(value, axis)]
    dot_general x4 -> x0, matrix products: 14.5 us -> none  [apply_gram(): jnp.einsum('ksi,kio->so', partial_value, panels, preferred_element_type=j...]
    all_to_all x2 -> x0, starting transfers between devices: 13.2 us -> none  [sum_at_owner(): lax.all_to_all(tiles, axis, split_axis=0, concat_axis=0, tiled=True)]
    another operation x6 -> x0, other arithmetic: 9.35 us -> none  [the longest x3 3.6 us: local(): factor = jnp.linalg.cholesky(precond)]
    reduce_sum x11 -> x0, other arithmetic: 8.67 us -> none  [the longest x4 3.96 us: sum_at_owner(): return arrived.sum(axis=0)]
  transfers between devices with their start and end apart: 6 -> 0, of which waited for: 5 -> 0; matrix products, arithmetic and copies ran while one was open for 4% -> 0% of each run, Pallas kernels for 0% -> 0%
where the time goes in v1:
time: 136 us
  Pallas kernels  131 us (96%)
  local copies, waits for them, and re-layouts  3.81 us (3%)
    pallas_call x1, Pallas kernels, local(): pl.pallas_call(kernel, out_shape=(jax.ShapeDtypeStruct((sub_rows, outs),...  131 us
    unnamed x5, local copies, waits for them, and re-layouts  3.19 us

profile of v1, /device:TPU:1, one launch (start us, length us, event | category | flops | bytes accessed | tf_op | source)
XLA Modules:
  0.0 135.7 jit_solution(4866199189940411331)
XLA Ops:
  0.6 0.0 copy-start
  0.6 1.6 %copy-done = bf16[4,8,1,32,1024]{4,3,2,1,0:T(8,128)(2,1)S(1)} copy-done((bf16[4,8,1,32,1024]{4,3,2,1,0:T(8,128)(2,1)S(1)}, bf16[4,8,1,32,1024]{4,3,2,1,0:T(8,128)(2,1)}, u32[]{:S(2)}) %copy-start) | copy-done | bytes 2097176
  2.2 0.0 copy-start.1
  2.2 0.9 copy-done.1
  3.2 131.2 %merge.1 = (f32[32,1024]{1,0:T(8,128)S(1)}, f32[8,128]{1,0:T(8,128)S(1)}) custom-call(bf16[4,256,1024]{2,1,0:T(8,128)(2,1)S(1)} %bitcast.1, bf16[4,32,1024]{2,1,0:T(8,128)(2,1)S(1)} %copy-done.1), custom_call_target="tpu_custom_call" | custom-call | tf_op jit(solution)/shard_map/merge/pallas_call | solution.py:378
  134.4 0.6 slice_reduce_fusion
  135.1 0.7 copy.5
Async XLA Ops:
  0.6 1.6 %copy-start = (bf16[4,8,1,32,1024]{4,3,2,1,0:T(8,128)(2,1)S(1)}, bf16[4,8,1,32,1024]{4,3,2,1,0:T(8,128)(2,1)}, u32[]{:S(2)}) copy-start(bf16[4,8,1,32,1024]{4,3,2,1,0:T(8,128)(2,1)} %param.2) | copy-start | bytes 6291460
  2.2 0.9 copy-start.1
